TPU v7x, 128 devices: a whole 4x4x4 slice. The times are simulated.
128 devices in a mesh: src: 8 (over z, core), tile: 16 (over x, y).
Axes of the slice: x: 4, y: 4, z: 4, core: 2. Of those that a mesh axis runs over, the one named last changes fastest.
Arguments:
- tables: float32 [128, 32, 32, 1024], P(('src', 'tile')), may hold values from 0.2 to 2
- weights: float32 [128, 32], P(('src', 'tile')), may hold values from 0.05 to 0.5
- aperture: int32 [128, 32], P(('src', 'tile')), may hold values from 0 to 1, as said below
Outputs:
- image: float32 [32, 64, 32, 128], P('tile', 'src')
Inputs may be any that keep to these rules, and one draw needn't show every extreme that they name: `aperture`: within one source and one group of 2 consecutive tiles (g * 2 to g * 2 + 1), at most 1 entries are 1; some group has exactly 1 for every source.
All inputs are finite; a program needn't handle non-finite values.
Results may differ from a plain program's by a relative error of at most 0.0003.
Values sent between devices are 32-bit elements; how exact they have to be, the bound alone decides.
A program may use at most 128 MiB of HBM per device.

v0:
```python
import jax
import jax.numpy as jnp
from jax import lax
from jax.sharding import PartitionSpec as P

BX = 32
BY = 16
BZ = 64


angular_rate = 9.0


def cut_along(array, dim, peers):
    shape = array.shape
    parts = array.reshape(*shape[:dim], peers, shape[dim] // peers, *shape[dim + 1 :])
    return jnp.moveaxis(parts, dim, 0)


def sent_and_summed(array, axis, dim):
    parts = cut_along(array, dim, lax.axis_size(axis))
    arrived = lax.all_to_all(parts, axis, split_axis=0, concat_axis=0, tiled=True)
    return arrived.sum(axis=0)


def refine_axis(values, axis):
    length = values.shape[axis]
    first = lax.slice_in_dim(values, 0, 1, axis=axis)
    last = lax.slice_in_dim(values, length - 1, length, axis=axis)
    lower = jnp.concatenate([first, lax.slice_in_dim(values, 0, length - 1, axis=axis)], axis=axis)
    upper = jnp.concatenate([lax.slice_in_dim(values, 1, length, axis=axis), last], axis=axis)
    even_rows = 0.75 * values + 0.25 * lower
    odd_rows = 0.75 * values + 0.25 * upper
    paired = jnp.stack([even_rows, odd_rows], axis=axis + 1)
    shape = values.shape[:axis] + (2 * length,) + values.shape[axis + 1 :]
    return paired.reshape(shape)


def refine_accumulate(coarse, details, fine_rows, tile_count):
    items = coarse.shape[0]
    turns = 8
    block = items // turns
    coarse_rows = coarse.shape[1]
    tile_ids = jnp.arange(tile_count).astype(jnp.float32)

    def one_block(total, item):
        bricks, info = item
        shaped = bricks.reshape(block, coarse_rows, BY, BZ)
        along_x = refine_axis(shaped, 1)
        along_z = refine_axis(along_x, 3)
        fine = refine_axis(along_z, 2)
        phase = jnp.cos(angular_rate * fine)
        select = (info[:, 1:2] == tile_ids[None, :]).astype(jnp.float32) * info[:, 0:1]
        total = total + jnp.einsum("kp,kfyz->pfyz", select, phase, precision=lax.Precision.HIGHEST)
        return (total, None)

    stacked = (
        coarse.reshape(turns, block, coarse_rows, coarse.shape[2]),
        details.reshape(turns, block, 2),
    )
    start = jnp.zeros((tile_count, fine_rows, 2 * BY, 2 * BZ), jnp.float32)
    total, unused = lax.scan(one_block, start, stacked)
    return total


def shards(tables, weights, aperture):
    bricks = tables[0]
    own_weight = weights[0]
    own_mask = aperture[0]
    owners = lax.axis_size("tile")
    group = bricks.shape[0] // owners
    capacity = group // 2
    plane = bricks.shape[2]
    live = own_mask.reshape(owners, group)
    ranking = jnp.cumsum(live, axis=1) - 1
    slot_ids = jnp.arange(capacity)
    chosen = ((live[:, None, :] == 1) & (ranking[:, None, :] == slot_ids[None, :, None])).astype(
        jnp.int32
    )
    local_tile = jnp.sum(chosen * jnp.arange(group)[None, None, :], axis=2)
    occupied = jnp.sum(chosen, axis=2)
    brick_index = local_tile + jnp.arange(owners)[:, None] * group
    picked = bricks[brick_index]
    factor = own_weight[brick_index] * occupied.astype(jnp.float32)
    details = jnp.stack([factor, local_tile.astype(jnp.float32)], axis=-1)
    arrived, info = (
        lax.all_to_all(picked, "tile", split_axis=0, concat_axis=0, tiled=True),
        lax.all_to_all(details, "tile", split_axis=0, concat_axis=0, tiled=True),
    )
    partial_image = refine_accumulate(
        arrived.reshape(-1, BX, plane), info.reshape(-1, 2), 2 * BX, group
    )
    image = sent_and_summed(partial_image, "src", 1)
    return image


def solution(mesh):
    placed = (
        P(("src", "tile"), None, None, None),
        P(("src", "tile"), None),
        P(("src", "tile"), None),
    )
    return jax.shard_map(
        shards, mesh=mesh, in_specs=placed, out_specs=P("tile", "src", None, None), check_vma=False
    )
```

profile of v0, /device:TPU:0, one launch (start us, length us, event | category | flops | bytes accessed | tf_op | source)
XLA Modules:
  0.0 492.8 jit_solution(5891532304846239543)
XLA Ops:
  4.4 7.1 %all-to-all-start = ((f32[16,1,2]{2,1,0:T(1,128)}), f32[16,1,2]{2,1,0:T(1,128)S(1)}, u32[]{:S(2)}, u32[]{:S(2)}) async-start(f32[16,1,2]{2,1,0:T(1,128)} %copy.101), calls=%async_computation | async-start | bytes 16384 | tf_op jit(solution)/shard_map/all_to_all | solution.py:88
  11.6 4.2 gather_fusion.1
  15.8 3.3 all-to-all-done
  19.1 3.9 all-to-all-start.1
  23.0 29.3 %all-to-all-done.1 = f32[16,1,32,1024]{3,2,1,0:T(8,128)S(1)} async-done(((f32[16,1,32,1024]{3,2,1,0:T(8,128)}), f32[16,1,32,1024]{3,2,1,0:T(8,128)S(1)}, u32[]{:S(2)}, u32[]{:S(2)}) %all-to-all-start.1) | async-done | bytes 2097184 | tf_op jit(solution)/shard_map/all_to_all | solution.py:87
  52.3 406.0 %while.11 = (s32[]{:T(128)}, f32[2,64,32,128]{3,0,2,1:T(2,128)}, f32[8,2,2]{2,1,0:T(2,128)S(1)}, f32[8,2,32,1024]{3,2,1,0:T(8,128)S(1)}, s32[]{:T(128)}, /*index=5*/s32[]{:T(128)}) while((s32[]{:T(128)}, f32[2,64,32,128]{3,0,2,1:T(2,128)}, f32[8,2,2]{2,1,0:T(2,128)S(1)}, f32[8,2,32,1024]{3,2,1,0:T(8,128)S(1)}, s32[]{:T(128)}, ...), condition=%wide.region_4.5_spmd.clone, body=%wide.region_3.4_spmd.clone.sunk | while | flops 18284556 | bytes 87916912 | solution.py:62
  63.3 2.9 copy.140
  66.1 2.6 copy.141
  68.7 3.2 copy.142
  74.6 3.7 copy.143
  82.4 6.7 %fusion.43 = f32[2,64,16,2,128]{4,2,3,1,0:T(8,128)S(1)} fusion(f32[2,64,16,1,128]{4,2,3,1,0:T(8,128)S(1)} %get-tuple-element.179, f32[2,64,16,1,128]{4,2,3,1,0:T(8,128)S(1)} %get-tuple-element.180), kind=kLoop, calls=%fused_computation.5.clone.1 | loop fusion | flops 1048576 | bytes 4194304 | tf_op jit(solution)/shard_map/while/body/eval_jaxpr/cos | solution.py:52
  90.7 10.9 %select_add_fusion.2 = f32[2,64,32,128]{3,0,2,1:T(2,128)S(1)} fusion(f32[2,64,32,128]{3,0,2,1:T(2,128)S(1)} %copy-done.5, pred[]{:T(512)S(6)} %compare.3, f32[2,64,32,128]{3,1,2,0:T(8,128)S(1)} %bitcast.100, f32[2]{0:T(128)S(1)} %get-tuple-element.181, f32[2]{0:T(128)S(1)} %get-tuple-element.182, f32[2]{0:T(128)S(1)} %iota_convert_fusion.2), kind=kOutput, calls=%fused_computation.6.clone.1 | convolution fusion | flops 13631496 | bytes 6291481 | tf_op jit(solution)/shard_map/while/body/eval_jaxpr/kp,kfyz->pfyz/dot_general | solution.py:54
  114.0 2.9 copy.140
  119.5 3.2 copy.142
  125.4 3.7 copy.143
  133.1 6.7 %fusion.43 = f32[2,64,16,2,128]{4,2,3,1,0:T(8,128)S(1)} fusion(f32[2,64,16,1,128]{4,2,3,1,0:T(8,128)S(1)} %get-tuple-element.179, f32[2,64,16,1,128]{4,2,3,1,0:T(8,128)S(1)} %get-tuple-element.180), kind=kLoop, calls=%fused_computation.5.clone.1 | loop fusion | flops 1048576 | bytes 4194304 | tf_op jit(solution)/shard_map/while/body/eval_jaxpr/cos | solution.py:52
  141.5 10.9 %select_add_fusion.2 = f32[2,64,32,128]{3,0,2,1:T(2,128)S(1)} fusion(f32[2,64,32,128]{3,0,2,1:T(2,128)S(1)} %copy-done.5, pred[]{:T(512)S(6)} %compare.3, f32[2,64,32,128]{3,1,2,0:T(8,128)S(1)} %bitcast.100, f32[2]{0:T(128)S(1)} %get-tuple-element.181, f32[2]{0:T(128)S(1)} %get-tuple-element.182, f32[2]{0:T(128)S(1)} %iota_convert_fusion.2), kind=kOutput, calls=%fused_computation.6.clone.1 | convolution fusion | flops 13631496 | bytes 6291481 | tf_op jit(solution)/shard_map/while/body/eval_jaxpr/kp,kfyz->pfyz/dot_general | solution.py:54
  164.8 2.9 copy.140
  170.2 3.2 copy.142
  176.1 3.7 copy.143
  183.9 6.7 %fusion.43 = f32[2,64,16,2,128]{4,2,3,1,0:T(8,128)S(1)} fusion(f32[2,64,16,1,128]{4,2,3,1,0:T(8,128)S(1)} %get-tuple-element.179, f32[2,64,16,1,128]{4,2,3,1,0:T(8,128)S(1)} %get-tuple-element.180), kind=kLoop, calls=%fused_computation.5.clone.1 | loop fusion | flops 1048576 | bytes 4194304 | tf_op jit(solution)/shard_map/while/body/eval_jaxpr/cos | solution.py:52
  192.2 11.0 %select_add_fusion.2 = f32[2,64,32,128]{3,0,2,1:T(2,128)S(1)} fusion(f32[2,64,32,128]{3,0,2,1:T(2,128)S(1)} %copy-done.5, pred[]{:T(512)S(6)} %compare.3, f32[2,64,32,128]{3,1,2,0:T(8,128)S(1)} %bitcast.100, f32[2]{0:T(128)S(1)} %get-tuple-element.181, f32[2]{0:T(128)S(1)} %get-tuple-element.182, f32[2]{0:T(128)S(1)} %iota_convert_fusion.2), kind=kOutput, calls=%fused_computation.6.clone.1 | convolution fusion | flops 13631496 | bytes 6291481 | tf_op jit(solution)/shard_map/while/body/eval_jaxpr/kp,kfyz->pfyz/dot_general | solution.py:54
  215.5 2.9 copy.140
  221.0 3.2 copy.142
  226.9 3.7 copy.143
  234.6 6.7 %fusion.43 = f32[2,64,16,2,128]{4,2,3,1,0:T(8,128)S(1)} fusion(f32[2,64,16,1,128]{4,2,3,1,0:T(8,128)S(1)} %get-tuple-element.179, f32[2,64,16,1,128]{4,2,3,1,0:T(8,128)S(1)} %get-tuple-element.180), kind=kLoop, calls=%fused_computation.5.clone.1 | loop fusion | flops 1048576 | bytes 4194304 | tf_op jit(solution)/shard_map/while/body/eval_jaxpr/cos | solution.py:52
  243.0 10.9 %select_add_fusion.2 = f32[2,64,32,128]{3,0,2,1:T(2,128)S(1)} fusion(f32[2,64,32,128]{3,0,2,1:T(2,128)S(1)} %copy-done.5, pred[]{:T(512)S(6)} %compare.3, f32[2,64,32,128]{3,1,2,0:T(8,128)S(1)} %bitcast.100, f32[2]{0:T(128)S(1)} %get-tuple-element.181, f32[2]{0:T(128)S(1)} %get-tuple-element.182, f32[2]{0:T(128)S(1)} %iota_convert_fusion.2), kind=kOutput, calls=%fused_computation.6.clone.1 | convolution fusion | flops 13631496 | bytes 6291481 | tf_op jit(solution)/shard_map/while/body/eval_jaxpr/kp,kfyz->pfyz/dot_general | solution.py:54
  266.3 2.9 copy.140
  271.7 3.2 copy.142
  277.6 3.7 copy.143
  285.4 6.7 %fusion.43 = f32[2,64,16,2,128]{4,2,3,1,0:T(8,128)S(1)} fusion(f32[2,64,16,1,128]{4,2,3,1,0:T(8,128)S(1)} %get-tuple-element.179, f32[2,64,16,1,128]{4,2,3,1,0:T(8,128)S(1)} %get-tuple-element.180), kind=kLoop, calls=%fused_computation.5.clone.1 | loop fusion | flops 1048576 | bytes 4194304 | tf_op jit(solution)/shard_map/while/body/eval_jaxpr/cos | solution.py:52
  293.7 10.9 %select_add_fusion.2 = f32[2,64,32,128]{3,0,2,1:T(2,128)S(1)} fusion(f32[2,64,32,128]{3,0,2,1:T(2,128)S(1)} %copy-done.5, pred[]{:T(512)S(6)} %compare.3, f32[2,64,32,128]{3,1,2,0:T(8,128)S(1)} %bitcast.100, f32[2]{0:T(128)S(1)} %get-tuple-element.181, f32[2]{0:T(128)S(1)} %get-tuple-element.182, f32[2]{0:T(128)S(1)} %iota_convert_fusion.2), kind=kOutput, calls=%fused_computation.6.clone.1 | convolution fusion | flops 13631496 | bytes 6291481 | tf_op jit(solution)/shard_map/while/body/eval_jaxpr/kp,kfyz->pfyz/dot_general | solution.py:54
  317.0 2.9 copy.140
  322.5 3.2 copy.142
  328.4 3.7 copy.143
  336.1 6.7 %fusion.43 = f32[2,64,16,2,128]{4,2,3,1,0:T(8,128)S(1)} fusion(f32[2,64,16,1,128]{4,2,3,1,0:T(8,128)S(1)} %get-tuple-element.179, f32[2,64,16,1,128]{4,2,3,1,0:T(8,128)S(1)} %get-tuple-element.180), kind=kLoop, calls=%fused_computation.5.clone.1 | loop fusion | flops 1048576 | bytes 4194304 | tf_op jit(solution)/shard_map/while/body/eval_jaxpr/cos | solution.py:52
  344.5 10.9 %select_add_fusion.2 = f32[2,64,32,128]{3,0,2,1:T(2,128)S(1)} fusion(f32[2,64,32,128]{3,0,2,1:T(2,128)S(1)} %copy-done.5, pred[]{:T(512)S(6)} %compare.3, f32[2,64,32,128]{3,1,2,0:T(8,128)S(1)} %bitcast.100, f32[2]{0:T(128)S(1)} %get-tuple-element.181, f32[2]{0:T(128)S(1)} %get-tuple-element.182, f32[2]{0:T(128)S(1)} %iota_convert_fusion.2), kind=kOutput, calls=%fused_computation.6.clone.1 | convolution fusion | flops 13631496 | bytes 6291481 | tf_op jit(solution)/shard_map/while/body/eval_jaxpr/kp,kfyz->pfyz/dot_general | solution.py:54
  367.8 2.9 copy.140
  373.2 3.2 copy.142
  379.1 3.7 copy.143
  386.9 6.7 %fusion.43 = f32[2,64,16,2,128]{4,2,3,1,0:T(8,128)S(1)} fusion(f32[2,64,16,1,128]{4,2,3,1,0:T(8,128)S(1)} %get-tuple-element.179, f32[2,64,16,1,128]{4,2,3,1,0:T(8,128)S(1)} %get-tuple-element.180), kind=kLoop, calls=%fused_computation.5.clone.1 | loop fusion | flops 1048576 | bytes 4194304 | tf_op jit(solution)/shard_map/while/body/eval_jaxpr/cos | solution.py:52
  395.2 10.9 %select_add_fusion.2 = f32[2,64,32,128]{3,0,2,1:T(2,128)S(1)} fusion(f32[2,64,32,128]{3,0,2,1:T(2,128)S(1)} %copy-done.5, pred[]{:T(512)S(6)} %compare.3, f32[2,64,32,128]{3,1,2,0:T(8,128)S(1)} %bitcast.100, f32[2]{0:T(128)S(1)} %get-tuple-element.181, f32[2]{0:T(128)S(1)} %get-tuple-element.182, f32[2]{0:T(128)S(1)} %iota_convert_fusion.2), kind=kOutput, calls=%fused_computation.6.clone.1 | convolution fusion | flops 13631496 | bytes 6291481 | tf_op jit(solution)/shard_map/while/body/eval_jaxpr/kp,kfyz->pfyz/dot_general | solution.py:54
  418.5 2.9 copy.140
  423.9 3.2 copy.142
  429.9 3.7 copy.143
  437.6 6.7 %fusion.43 = f32[2,64,16,2,128]{4,2,3,1,0:T(8,128)S(1)} fusion(f32[2,64,16,1,128]{4,2,3,1,0:T(8,128)S(1)} %get-tuple-element.179, f32[2,64,16,1,128]{4,2,3,1,0:T(8,128)S(1)} %get-tuple-element.180), kind=kLoop, calls=%fused_computation.5.clone.1 | loop fusion | flops 1048576 | bytes 4194304 | tf_op jit(solution)/shard_map/while/body/eval_jaxpr/cos | solution.py:52
  446.0 10.9 %select_add_fusion.2 = f32[2,64,32,128]{3,0,2,1:T(2,128)S(1)} fusion(f32[2,64,32,128]{3,0,2,1:T(2,128)S(1)} %copy-done.5, pred[]{:T(512)S(6)} %compare.3, f32[2,64,32,128]{3,1,2,0:T(8,128)S(1)} %bitcast.100, f32[2]{0:T(128)S(1)} %get-tuple-element.181, f32[2]{0:T(128)S(1)} %get-tuple-element.182, f32[2]{0:T(128)S(1)} %iota_convert_fusion.2), kind=kOutput, calls=%fused_computation.6.clone.1 | convolution fusion | flops 13631496 | bytes 6291481 | tf_op jit(solution)/shard_map/while/body/eval_jaxpr/kp,kfyz->pfyz/dot_general | solution.py:54
  458.3 32.5 %all_to_all.15 = f32[8,2,8,32,128]{4,1,3,2,0:T(2,128)S(1)} all-to-all(f32[8,2,8,32,128]{4,1,3,2,0:T(2,128)} %bitcast.104), channel_id=1, replica_groups=mesh['src'=8,'tile'=16] {'src'}, dimensions={0} | all-to-all | bytes 4194304 | tf_op jit(solution)/shard_map/all_to_all | solution.py:22
  (338 shorter events, 188.8 us)
Async XLA Ops:
  0.0 3.0 copy-start
  4.4 14.7 %all-to-all-start = ((f32[16,1,2]{2,1,0:T(1,128)}), f32[16,1,2]{2,1,0:T(1,128)S(1)}, u32[]{:S(2)}, u32[]{:S(2)}) async-start(f32[16,1,2]{2,1,0:T(1,128)} %copy.101), calls=%async_computation | async-start | bytes 16384 | tf_op jit(solution)/shard_map/all_to_all | solution.py:88
  19.1 33.2 %all-to-all-start.1 = ((f32[16,1,32,1024]{3,2,1,0:T(8,128)}), f32[16,1,32,1024]{3,2,1,0:T(8,128)S(1)}, u32[]{:S(2)}, u32[]{:S(2)}) async-start(f32[16,1,32,1024]{3,2,1,0:T(8,128)} %bitcast.7), calls=%async_computation.1 | async-start | bytes 4194304 | tf_op jit(solution)/shard_map/all_to_all | solution.py:87
  52.3 1.3 copy-start.3
  59.8 1.2 copy-start.2
  74.6 3.7 copy-start.1
  89.2 1.6 copy-start.5
  90.7 12.3 %copy-start.4 = (f32[8,2,32,1024]{3,2,1,0:T(8,128)S(1)}, f32[8,2,32,1024]{3,2,1,0:T(8,128)}, u32[]{:S(2)}) copy-start(f32[8,2,32,1024]{3,2,1,0:T(8,128)} %copy-done.3) | copy-start | bytes 6291460 | tf_op jit(solution)/shard_map/while
  101.7 1.3 copy-start.6
  103.1 1.3 copy-start.3
  110.5 1.2 copy-start.2
  125.4 3.7 copy-start.1
  139.9 1.6 copy-start.5
  141.5 12.3 %copy-start.4 = (f32[8,2,32,1024]{3,2,1,0:T(8,128)S(1)}, f32[8,2,32,1024]{3,2,1,0:T(8,128)}, u32[]{:S(2)}) copy-start(f32[8,2,32,1024]{3,2,1,0:T(8,128)} %copy-done.3) | copy-start | bytes 6291460 | tf_op jit(solution)/shard_map/while
  152.4 1.3 copy-start.6
  153.8 1.3 copy-start.3
  161.3 1.2 copy-start.2
  176.1 3.7 copy-start.1
  190.6 1.6 copy-start.5
  192.2 12.3 %copy-start.4 = (f32[8,2,32,1024]{3,2,1,0:T(8,128)S(1)}, f32[8,2,32,1024]{3,2,1,0:T(8,128)}, u32[]{:S(2)}) copy-start(f32[8,2,32,1024]{3,2,1,0:T(8,128)} %copy-done.3) | copy-start | bytes 6291460 | tf_op jit(solution)/shard_map/while
  203.2 1.3 copy-start.6
  204.6 1.3 copy-start.3
  212.0 1.2 copy-start.2
  226.9 3.7 copy-start.1
  241.4 1.6 copy-start.5
  243.0 12.3 %copy-start.4 = (f32[8,2,32,1024]{3,2,1,0:T(8,128)S(1)}, f32[8,2,32,1024]{3,2,1,0:T(8,128)}, u32[]{:S(2)}) copy-start(f32[8,2,32,1024]{3,2,1,0:T(8,128)} %copy-done.3) | copy-start | bytes 6291460 | tf_op jit(solution)/shard_map/while
  253.9 1.3 copy-start.6
  255.3 1.3 copy-start.3
  262.8 1.2 copy-start.2
  277.6 3.7 copy-start.1
  292.1 1.6 copy-start.5
  293.7 12.3 %copy-start.4 = (f32[8,2,32,1024]{3,2,1,0:T(8,128)S(1)}, f32[8,2,32,1024]{3,2,1,0:T(8,128)}, u32[]{:S(2)}) copy-start(f32[8,2,32,1024]{3,2,1,0:T(8,128)} %copy-done.3) | copy-start | bytes 6291460 | tf_op jit(solution)/shard_map/while
  304.7 1.3 copy-start.6
  306.0 1.3 copy-start.3
  328.4 3.7 copy-start.1
  342.9 1.6 copy-start.5
  344.5 12.3 %copy-start.4 = (f32[8,2,32,1024]{3,2,1,0:T(8,128)S(1)}, f32[8,2,32,1024]{3,2,1,0:T(8,128)}, u32[]{:S(2)}) copy-start(f32[8,2,32,1024]{3,2,1,0:T(8,128)} %copy-done.3) | copy-start | bytes 6291460 | tf_op jit(solution)/shard_map/while
  355.4 1.3 copy-start.6
  356.8 1.3 copy-start.3
  379.1 3.7 copy-start.1
  393.6 1.6 copy-start.5
  395.2 12.3 %copy-start.4 = (f32[8,2,32,1024]{3,2,1,0:T(8,128)S(1)}, f32[8,2,32,1024]{3,2,1,0:T(8,128)}, u32[]{:S(2)}) copy-start(f32[8,2,32,1024]{3,2,1,0:T(8,128)} %copy-done.3) | copy-start | bytes 6291460 | tf_op jit(solution)/shard_map/while
  406.2 1.3 copy-start.6
  407.5 1.3 copy-start.3
  429.9 3.7 copy-start.1
  444.4 1.6 copy-start.5
  446.0 12.3 %copy-start.4 = (f32[8,2,32,1024]{3,2,1,0:T(8,128)S(1)}, f32[8,2,32,1024]{3,2,1,0:T(8,128)}, u32[]{:S(2)}) copy-start(f32[8,2,32,1024]{3,2,1,0:T(8,128)} %copy-done.3) | copy-start | bytes 6291460 | tf_op jit(solution)/shard_map/while
  456.9 1.3 copy-start.6
  (3 other events, 3.7 us)
where the time goes:
time: 495 us; the launch traced here: 493 us
  local copies, waits for them, and re-layouts  233 us (47%)
  other arithmetic  94.4 us (19%)
  matrix products  87.6 us (18%)
  waiting for transfers between devices  32.6 us (7%)
  blocking collectives  32.5 us (7%)
  starting transfers between devices  11.1 us (2%)
    dot_general x8, matrix products, one_block(): jnp.einsum('kp,kfyz->pfyz', select, phase, precision=lax.Precision.HIGHEST)  87.6 us
    while x128, local copies, waits for them, and re-layouts  74.1 us
    cos x8, other arithmetic, one_block(): phase = jnp.cos(angular_rate * fine)  54 us
    mul x32, local copies, waits for them, and re-layouts, refine_axis(): even_rows = 0.75 * values + 0.25 * lower  45.7 us
    all_to_all x1, blocking collectives, sent_and_summed(): lax.all_to_all(parts, axis, split_axis=0, concat_axis=0, tiled=True)  32.5 us
    all_to_all x1, waiting for transfers between devices, shards(): lax.all_to_all(picked, 'tile', split_axis=0, concat_axis=0, tiled=True)  29.3 us
    another operation x16, local copies, waits for them, and re-layouts, refine_axis(): paired = jnp.stack([even_rows, odd_rows], axis=axis + 1)  26.5 us
    slice x24, local copies, waits for them, and re-layouts, refine_axis(): first = lax.slice_in_dim(values, 0, 1, axis=axis)  25.5 us
  transfers between devices with their start and end apart: 2, of which 2 were waited for; matrix products, arithmetic and copies ran while one was open for 1% of the time, Pallas kernels for 0%

commit v1 on v0

v1 whole, which is shorter than its diff:
```python
import functools
import math

import jax
import jax.numpy as jnp
from jax import lax
from jax.experimental import pallas as pl
from jax.experimental.pallas import tpu as pltpu
from jax.sharding import PartitionSpec as P

BY = 16
BZ = 64
SUB = 8
LANES = 128
ROWS = 32
DEPTH = 16
COMPS = 4
PIECES = 2
KK = 4

angular_rate = 9.0
MESH = pl.DeviceIdType.MESH

CHUNKS = (
    (6, 0, 4),
    (4, 6, 0),
    (6, 10, 12),
    (2, 16, 10),
    (6, 18, 20),
    (2, 24, 18),
    (4, 26, 28),
    (2, 30, 26),
)


def sine_coefficients():
    import numpy as np

    n = 4
    k = np.arange(4000)
    r = 0.5 * np.cos((k + 0.5) * np.pi / 8000)
    powers = np.stack([r ** (2 * i + 1) for i in range(n)], axis=1)
    weight = 1.0 / np.sqrt(np.sin((k + 0.5) * np.pi / 8000) + 1e-3)
    target = np.sin(np.pi * r)
    for _ in range(60):
        got, *_rest = np.linalg.lstsq(powers * weight[:, None], target * weight, rcond=None)
        err = np.abs(powers @ got - target)
        weight = weight * (0.5 + 0.5 * err / err.max()) ** 0.5
        weight = weight / weight.max()
    return [float(np.float32(math.sqrt(2.0) * c)) for c in got]


def lane_masks(shape):
    lane = lax.broadcasted_iota(jnp.int32, shape, len(shape) - 1)
    sub = lax.broadcasted_iota(jnp.int32, shape, len(shape) - 2)
    z = lane & (BZ - 1)
    low = lane < BZ
    return z == 0, z == BZ - 1, low, low & (sub == 0), jnp.logical_not(low) & (sub == SUB - 1)


def kernel(
    coeffs,
    tables,
    weights,
    aperture,
    out,
    raw,
    send,
    recv,
    info_send,
    info_recv,
    splat,
    total_weight,
    fine,
    sib_send,
    sib_recv,
    far_send,
    far_recv,
    final,
    perm,
    load_sem,
    send_sem,
    recv_sem,
    info_ssem,
    info_rsem,
    sib_ssem,
    sib_rsem,
    far_ssem,
    far_rsem,
):
    a = lax.axis_index("src")
    t = lax.axis_index("tile")
    z, c = a // 2, a % 2
    tx, ty = t // 4, t % 4

    def owner_of(d):
        return ((tx + d // 4) % 4) * 4 + (ty + d % 4) % 4

    def load(i):
        first = pl.multiple_of(((z + 1 + i) % 4) * SUB, SUB)
        return pltpu.make_async_copy(
            tables.at[0, :, pl.ds(first, SUB), :], raw.at[i], load_sem.at[i]
        )

    for i in range(4):
        load(i).start()

    bar = pltpu.get_barrier_semaphore()

    def greet(d, carry):
        pl.semaphore_signal(bar, inc=1, device_id={"tile": owner_of(d), "src": a}, device_id_type=MESH)
        return carry

    lax.fori_loop(1, DEPTH, greet, 0)
    sibling = 2 * z + 1 - c
    pl.semaphore_signal(bar, inc=1, device_id={"src": sibling, "tile": t}, device_id_type=MESH)
    for m in range(3):
        far = 2 * ((z + 1 + m) % 4) + c
        pl.semaphore_signal(bar, inc=1, device_id={"src": far, "tile": t}, device_id_type=MESH)

    def fill_info(d, carry):
        first = 2 * owner_of(d)
        for j in range(2):
            w = jnp.full((SUB, LANES), weights[0, first + j], jnp.float32)
            live = jnp.full((SUB, LANES), aperture[0, first + j], jnp.int32)
            info_send[d, j] = w * live.astype(jnp.float32)
        return carry

    lax.fori_loop(0, DEPTH, fill_info, 0)

    def pick(i):
        def one(d, carry):
            first = 2 * owner_of(d)
            second = jnp.full((SUB, LANES), aperture[0, first + 1], jnp.int32) == 1
            for k in range(8):
                lanes = pl.ds(k * LANES, LANES)
                chosen = jnp.where(second, raw[i, first + 1, :, lanes], raw[i, first, :, lanes])
                send[d, pl.ds((1 + 8 * i) * SUB + k, SUB, stride=SUB), :] = chosen
            return carry

        lax.fori_loop(0, DEPTH, one, 0)

    load(0).wait()
    pick(0)
    load(3).wait()
    pick(3)

    def wrap(d, carry):
        send[d, pl.ds(0, SUB), :] = send[d, pl.ds(32 * SUB, SUB), :]
        return carry

    lax.fori_loop(0, DEPTH, wrap, 0)
    load(1).wait()
    pick(1)

    pl.semaphore_wait(bar, DEPTH - 1 + 4)

    def rows_of(n):
        size, start1, start0 = CHUNKS[n]
        start = start0 + (start1 - start0) * c
        return pl.ds(pl.multiple_of(start * SUB, SUB), size * SUB)

    def send_info(d, carry):
        pltpu.make_async_remote_copy(
            info_send.at[d], info_recv.at[d], info_ssem, info_rsem,
            device_id={"tile": owner_of(d), "src": a}, device_id_type=MESH,
        ).start()
        return carry

    def send_chunk(n):
        rows = rows_of(n)

        def one(d, carry):
            pltpu.make_async_remote_copy(
                send.at[d, rows], recv.at[d, rows], send_sem.at[n], recv_sem.at[n],
                device_id={"tile": owner_of(d), "src": a}, device_id_type=MESH,
            ).start()
            return carry

        lax.fori_loop(1, DEPTH, one, 0)

    def own_chunk(n):
        rows = rows_of(n)
        recv[0, rows, :] = send[0, rows, :]

    lax.fori_loop(1, DEPTH, send_info, 0)
    send_chunk(0)
    send_chunk(1)
    load(2).wait()
    pick(2)
    for n in range(2, 8):
        send_chunk(n)
    for n in range(8):
        own_chunk(n)

    row = lax.broadcasted_iota(jnp.int32, (2 * LANES, 2 * LANES), 0)
    col = lax.broadcasted_iota(jnp.int32, (2 * LANES, 2 * LANES), 1)
    place = ((row // BZ) % 2) * LANES + 2 * (row % BZ) + row // LANES
    perm[...] = (col == place).astype(jnp.float32).astype(jnp.bfloat16)

    info_send_bytes = info_send.at[pl.ds(1, DEPTH - 1)]
    pltpu.make_async_copy(
        info_send_bytes, info_recv.at[pl.ds(1, DEPTH - 1)], info_rsem
    ).wait()
    splat[0] = info_send[0]
    splat[pl.ds(1, DEPTH - 1)] = info_recv[pl.ds(1, DEPTH - 1)]
    total_weight[...] = jnp.sum(splat[...], axis=0)

    scale = angular_rate / (2.0 * math.pi) / 64.0
    group = 4

    def refine_rows(n):
        size, start1, start0 = CHUNKS[n]
        start = start0 + (start1 - start0) * c
        z_first, z_last, low, y_first, y_last = lane_masks((group, SUB, LANES))

        def one(i, carry):
            q = start + i // (DEPTH // group)
            s = (i % (DEPTH // group)) * group
            base = recv[pl.ds(s, group), pl.ds(pl.multiple_of(q * SUB, SUB), SUB), :] * scale
            triple = 3.0 * base
            below = jnp.where(z_first, base, pltpu.roll(base, 1, 2))
            above = jnp.where(z_last, base, pltpu.roll(base, LANES - 1, 2))
            for pz, v in enumerate((triple + below, triple + above)):
                swap = pltpu.roll(v, BZ, 2)
                down = pltpu.roll(swap, 1, 1)
                up = pltpu.roll(swap, SUB - 1, 1)
                before = jnp.where(y_first, v, jnp.where(low, down, swap))
                after = jnp.where(y_last, v, jnp.where(low, swap, up))
                v3 = 3.0 * v
                fine[q, pl.ds(s, group), pz] = v3 + before
                fine[q, pl.ds(s, group), 2 + pz] = v3 + after
            return carry

        lax.fori_loop(0, size * (DEPTH // group), one, 0)

    c0, c1, c2, c3 = coeffs

    def piece_rows(p):
        return pl.ds(p * (8 // PIECES), 8 // PIECES)

    def partial_rows(m, half, target, p):
        low_q = 8 * m + 4 * half
        owner = 2 * ((z + 1 + m) % 4) + half
        at_first = (owner == 0).astype(jnp.int32)
        at_last = (owner == 7).astype(jnp.int32)
        per = KK // PIECES

        def one_row(kk, carry):
            k = (low_q + 1 + kk) % ROWS
            prev = (low_q + kk + at_first * (kk == 0).astype(jnp.int32)) % ROWS
            following = (low_q + 2 + kk - at_last * (kk == KK - 1).astype(jnp.int32)) % ROWS

            def some_sources(g, acc):
                acc = list(acc)
                for u in range(2):
                    s = g * 2 + u
                    f0 = splat[s, 0]
                    f1 = splat[s, 1]
                    for comp in range(COMPS):
                        center = 3.0 * fine[k, s, comp]
                        for par, other in enumerate((prev, following)):
                            phase = center + fine[other, s, comp]
                            r = phase - lax.round(phase, lax.RoundingMethod.TO_NEAREST_EVEN)
                            sq = r * r
                            root = r * (((c3 * sq + c2) * sq + c1) * sq + c0)
                            val = root * root
                            at = par * 8 + comp
                            acc[at] = acc[at] + f0 * val
                            acc[at + 4] = acc[at + 4] + f1 * val
                return tuple(acc)

            zero = jnp.zeros((SUB, LANES), jnp.float32)
            acc = lax.fori_loop(0, DEPTH // 2, some_sources, (zero,) * 16)
            for par in range(2):
                for tile in range(2):
                    for comp in range(COMPS):
                        target[2 * kk + par, tile, comp] = (
                            total_weight[tile] - acc[par * 8 + tile * 4 + comp]
                        )
            return carry

        lax.fori_loop(p * per, (p + 1) * per, one_row, 0)

    def to_sibling(m, p):
        return pltpu.make_async_remote_copy(
            sib_send.at[m, piece_rows(p)], sib_recv.at[m, piece_rows(p)],
            sib_ssem.at[m, p], sib_rsem.at[m, p],
            device_id={"src": sibling, "tile": t}, device_id_type=MESH,
        )

    def to_owner(m, p):
        far = 2 * ((z + 1 + m) % 4) + c
        return pltpu.make_async_remote_copy(
            far_send.at[m, piece_rows(p)], far_recv.at[m, piece_rows(p)],
            far_ssem.at[m, p], far_rsem.at[m, p],
            device_id={"src": far, "tile": t}, device_id_type=MESH,
        )

    def wait_chunk(n):
        rows = rows_of(n)
        pltpu.make_async_copy(
            send.at[pl.ds(1, DEPTH - 1), rows], recv.at[pl.ds(1, DEPTH - 1), rows], recv_sem.at[n]
        ).wait()

    for m in range(4):
        wait_chunk(2 * m)
        refine_rows(2 * m)
        for p in range(PIECES):
            partial_rows(m, 1 - c, sib_send.at[m], p)
            to_sibling(m, p).start()
        wait_chunk(2 * m + 1)
        refine_rows(2 * m + 1)
        mine = far_send.at[m] if m < 3 else final
        for p in range(PIECES):
            partial_rows(m, c, mine, p)
            to_sibling(m, p).wait_recv()
            if m < 3:

                def add_sibling(x, carry):
                    far_send[m, x] = far_send[m, x] + sib_recv[m, x]
                    return carry

                lax.fori_loop(p * (8 // PIECES), (p + 1) * (8 // PIECES), add_sibling, 0)
                to_owner(m, p).start()

    for m in range(3):
        for p in range(PIECES):
            to_owner(m, p).wait_recv()

    for par in range(2):

        def finish(x, carry):
            for tile in range(2):
                for comp in range(2):
                    at = 2 * par + comp
                    got = final[x, tile, at] + sib_recv[3, x, tile, at]
                    for m in range(3):
                        got = got + far_recv[m, x, tile, at]
                    final[x, tile, at] = got
            return carry

        lax.fori_loop(0, 8, finish, 0)

    halves = [
        jnp.concatenate(
            [final[:, :, pl.ds(2 * par, 1)].reshape(16 * SUB, LANES),
             final[:, :, pl.ds(2 * par + 1, 1)].reshape(16 * SUB, LANES)], axis=1)
        for par in range(2)
    ]
    for par in range(2):
        value = halves[par]
        mixed = jnp.zeros((16 * SUB, 2 * LANES), jnp.float32)
        for _ in range(3):
            part = value.astype(jnp.bfloat16)
            value = value - part.astype(jnp.float32)
            mixed = mixed + jnp.dot(part, perm[...], preferred_element_type=jnp.float32)
        for x in range(8):
            for tile in range(2):
                at = (x * 2 + tile) * SUB
                for h in range(2):
                    out[tile, x, pl.ds(2 * h + par, SUB, stride=4), :] = (
                        mixed[at : at + SUB, h * LANES : (h + 1) * LANES]
                    )

    pltpu.make_async_copy(
        info_send_bytes, info_recv.at[pl.ds(1, DEPTH - 1)], info_ssem
    ).wait()
    for n in range(8):
        rows = rows_of(n)
        pltpu.make_async_copy(
            send.at[pl.ds(1, DEPTH - 1), rows], recv.at[pl.ds(1, DEPTH - 1), rows], send_sem.at[n]
        ).wait()
    for m in range(4):
        for p in range(PIECES):
            to_sibling(m, p).wait_send()
            if m < 3:
                to_owner(m, p).wait_send()


def shards(tables, weights, aperture):
    part = (8, 2, COMPS, SUB, LANES)
    vmem = pltpu.VMEM
    f32 = jnp.float32
    dma = pltpu.SemaphoreType.DMA
    return pl.pallas_call(
        functools.partial(kernel, sine_coefficients()),
        out_shape=jax.ShapeDtypeStruct((2, 8, 2 * BY, 2 * BZ), f32),
        in_specs=[
            pl.BlockSpec(memory_space=pl.ANY),
            pl.BlockSpec(memory_space=pltpu.SMEM),
            pl.BlockSpec(memory_space=pltpu.SMEM),
        ],
        out_specs=pl.BlockSpec(memory_space=pltpu.VMEM),
        scratch_shapes=[
            vmem((4, 32, SUB, 1024), f32),
            vmem((DEPTH, 33 * SUB, LANES), f32),
            vmem((DEPTH, ROWS * SUB, LANES), f32),
            vmem((DEPTH, 2, SUB, LANES), f32),
            vmem((DEPTH, 2, SUB, LANES), f32),
            vmem((DEPTH, 2, SUB, LANES), f32),
            vmem((2, SUB, LANES), f32),
            vmem((ROWS, DEPTH, COMPS, SUB, LANES), f32),
            vmem((4,) + part, f32),
            vmem((4,) + part, f32),
            vmem((3,) + part, f32),
            vmem((3,) + part, f32),
            vmem(part, f32),
            vmem((2 * LANES, 2 * LANES), jnp.bfloat16),
            dma((4,)),
            dma((8,)),
            dma((8,)),
            dma,
            dma,
            dma((4, PIECES)),
            dma((4, PIECES)),
            dma((3, PIECES)),
            dma((3, PIECES)),
        ],
        compiler_params=pltpu.CompilerParams(
            collective_id=0, has_side_effects=True, vmem_limit_bytes=60 * 2**20
        ),
    )(tables, weights, aperture)


def solution(mesh):
    placed = (
        P(("src", "tile"), None, None, None),
        P(("src", "tile"), None),
        P(("src", "tile"), None),
    )
    return jax.shard_map(
        shards, mesh=mesh, in_specs=placed, out_specs=P("tile", "src", None, None), check_vma=False
    )
```

time: 495 us -> 52.7 us (0.11)
  local copies, waits for them, and re-layouts: 233 us -> 1.67 us
  other arithmetic: 94.4 us -> 0 us
  matrix products: 87.6 us -> 0 us
  Pallas kernels: 0 us -> 50.9 us
  waiting for transfers between devices: 32.6 us -> 0 us
  blocking collectives: 32.5 us -> 0 us
  starting transfers between devices: 11.1 us -> 0 us
    dot_general x8 -> x0, matrix products: 87.6 us -> none  [one_block(): jnp.einsum('kp,kfyz->pfyz', select, phase, precision=lax.Precision.HIGHEST)]
    while x128 -> x0, local copies, waits for them, and re-layouts: 74.1 us -> none
    cos x8 -> x0, other arithmetic: 54 us -> none  [one_block(): phase = jnp.cos(angular_rate * fine)]
    pallas_call x0 -> x1, Pallas kernels: none -> 50.9 us  [shards(): pl.pallas_call(functools.partial(kernel, sine_coefficients()), out_shape=...]
    slice x48 -> x0, local copies, waits for them, and re-layouts: 49.8 us -> none  [the longest x24 25.5 us: refine_axis(): first = lax.slice_in_dim(values, 0, 1, axis=axis)]
    mul x32 -> x0, local copies, waits for them, and re-layouts: 45.7 us -> none  [refine_axis(): even_rows = 0.75 * values + 0.25 * lower]
    all_to_all x2 -> x0, waiting for transfers between devices: 32.6 us -> none  [the longest x1 29.3 us: shards(): lax.all_to_all(picked, 'tile', split_axis=0, concat_axis=0, tiled=True)]
    all_to_all x1 -> x0, blocking collectives: 32.5 us -> none  [sent_and_summed(): lax.all_to_all(parts, axis, split_axis=0, concat_axis=0, tiled=True)]
  transfers between devices with their start and end apart: 2 -> 0, of which waited for: 2 -> 0; matrix products, arithmetic and copies ran while one was open for 1% -> 0% of each run, Pallas kernels for 0% -> 0%
where the time goes in v1:
time: 52.7 us; the launch traced here: 52.6 us
  Pallas kernels  50.9 us (97%)
  local copies, waits for them, and re-layouts  1.67 us (3%)
    pallas_call x1, Pallas kernels, shards(): pl.pallas_call(functools.partial(kernel, sine_coefficients()), out_shape=...  50.9 us
    unnamed x1, local copies, waits for them, and re-layouts  1.67 us

profile of v1, /device:TPU:0, one launch (start us, length us, event | category | flops | bytes accessed | tf_op | source)
XLA Modules:
  0.0 52.6 jit_solution(5388281676347714361)
XLA Ops:
  0.0 50.9 %shard_map.37 = f32[2,8,32,128]{3,2,1,0:T(8,128)} custom-call(f32[1,32,32,1024]{3,2,1,0:T(8,128)} %tables.1, f32[1,32]{1,0:T(1,128)} %weights.1, s32[1,32]{1,0:T(1,128)} %aperture.1), custom_call_target="tpu_custom_call" | custom-call | tf_op jit(solution)/shard_map/pallas_call | solution.py:386
  50.9 1.7 %copy.5 = f32[2,8,32,128]{3,2,1,0:T(8,128)} copy(f32[2,8,32,128]{3,2,1,0:T(8,128)} %shard_map.37) | data formatting | bytes 524288

commit v2 on v1

--- a/solution.py
+++ b/solution.py
@@ -128,6 +128,8 @@
 
     lax.fori_loop(0, DEPTH, fill_info, 0)
 
+    scale = angular_rate / (2.0 * math.pi) / 64.0
+
     def pick(i):
         def one(d, carry):
             first = 2 * owner_of(d)
@@ -135,7 +137,7 @@
             for k in range(8):
                 lanes = pl.ds(k * LANES, LANES)
                 chosen = jnp.where(second, raw[i, first + 1, :, lanes], raw[i, first, :, lanes])
-                send[d, pl.ds((1 + 8 * i) * SUB + k, SUB, stride=SUB), :] = chosen
+                send[d, pl.ds((1 + 8 * i) * SUB + k, SUB, stride=SUB), :] = chosen * scale
             return carry
 
         lax.fori_loop(0, DEPTH, one, 0)
@@ -206,33 +208,35 @@
     splat[pl.ds(1, DEPTH - 1)] = info_recv[pl.ds(1, DEPTH - 1)]
     total_weight[...] = jnp.sum(splat[...], axis=0)
 
-    scale = angular_rate / (2.0 * math.pi) / 64.0
-    group = 4
-
     def refine_rows(n):
         size, start1, start0 = CHUNKS[n]
         start = start0 + (start1 - start0) * c
-        z_first, z_last, low, y_first, y_last = lane_masks((group, SUB, LANES))
+        z_first, z_last, low, y_first, y_last = lane_masks((SUB, LANES))
 
         def one(i, carry):
-            q = start + i // (DEPTH // group)
-            s = (i % (DEPTH // group)) * group
-            base = recv[pl.ds(s, group), pl.ds(pl.multiple_of(q * SUB, SUB), SUB), :] * scale
-            triple = 3.0 * base
-            below = jnp.where(z_first, base, pltpu.roll(base, 1, 2))
-            above = jnp.where(z_last, base, pltpu.roll(base, LANES - 1, 2))
-            for pz, v in enumerate((triple + below, triple + above)):
-                swap = pltpu.roll(v, BZ, 2)
-                down = pltpu.roll(swap, 1, 1)
-                up = pltpu.roll(swap, SUB - 1, 1)
-                before = jnp.where(y_first, v, jnp.where(low, down, swap))
-                after = jnp.where(y_last, v, jnp.where(low, swap, up))
-                v3 = 3.0 * v
-                fine[q, pl.ds(s, group), pz] = v3 + before
-                fine[q, pl.ds(s, group), 2 + pz] = v3 + after
+            q = start + i
+            for s in range(DEPTH):
+                base = recv[s, pl.ds(pl.multiple_of(q * SUB, SUB), SUB), :]
+                swap = pltpu.roll(base, BZ, 1)
+                below = jnp.where(z_first, base, pltpu.roll(base, 1, 1))
+                above = jnp.where(z_last, base, pltpu.roll(base, LANES - 1, 1))
+                swap_below = jnp.where(z_first, swap, pltpu.roll(base, BZ + 1, 1))
+                swap_above = jnp.where(z_last, swap, pltpu.roll(base, BZ - 1, 1))
+                triple = 3.0 * base
+                swap_triple = 3.0 * swap
+                for pz in range(2):
+                    v = triple + (above if pz else below)
+                    w = swap_triple + (swap_above if pz else swap_below)
+                    down = pltpu.roll(w, 1, 0)
+                    up = pltpu.roll(w, SUB - 1, 0)
+                    before = jnp.where(y_first, v, jnp.where(low, down, w))
+                    after = jnp.where(y_last, v, jnp.where(low, w, up))
+                    v3 = 3.0 * v
+                    fine[q, s, pz] = v3 + before
+                    fine[q, s, 2 + pz] = v3 + after
             return carry
 
-        lax.fori_loop(0, size * (DEPTH // group), one, 0)
+        lax.fori_loop(0, size, one, 0)
 
     c0, c1, c2, c3 = coeffs
 
@@ -253,8 +257,8 @@
 
             def some_sources(g, acc):
                 acc = list(acc)
-                for u in range(2):
-                    s = g * 2 + u
+                for u in range(4):
+                    s = g * 4 + u
                     f0 = splat[s, 0]
                     f1 = splat[s, 1]
                     for comp in range(COMPS):
@@ -271,7 +275,7 @@
                 return tuple(acc)
 
             zero = jnp.zeros((SUB, LANES), jnp.float32)
-            acc = lax.fori_loop(0, DEPTH // 2, some_sources, (zero,) * 16)
+            acc = lax.fori_loop(0, DEPTH // 4, some_sources, (zero,) * 16)
             for par in range(2):
                 for tile in range(2):
                     for comp in range(COMPS):

time: 52.7 us -> 44.9 us (0.85)
  the two profiles are of different devices: /device:TPU:0 before, /device:TPU:33 now
where the time goes in v2:
time: 44.9 us; the launch traced here: 44.8 us
  Pallas kernels  43.1 us (96%)
  local copies, waits for them, and re-layouts  1.67 us (4%)
    pallas_call x1, Pallas kernels, shards(): pl.pallas_call(functools.partial(kernel, sine_coefficients()), out_shape=...  43.1 us
    unnamed x1, local copies, waits for them, and re-layouts  1.67 us

profile of v2, /device:TPU:33, one launch (start us, length us, event | category | flops | bytes accessed | tf_op | source)
XLA Modules:
  0.0 44.8 jit_solution(12153440524925671332)
XLA Ops:
  0.0 43.1 %shard_map.37 = f32[2,8,32,128]{3,2,1,0:T(8,128)} custom-call(f32[1,32,32,1024]{3,2,1,0:T(8,128)} %tables.1, f32[1,32]{1,0:T(1,128)} %weights.1, s32[1,32]{1,0:T(1,128)} %aperture.1), custom_call_target="tpu_custom_call" | custom-call | tf_op jit(solution)/shard_map/pallas_call | solution.py:390
  43.1 1.7 %copy.5 = f32[2,8,32,128]{3,2,1,0:T(8,128)} copy(f32[2,8,32,128]{3,2,1,0:T(8,128)} %shard_map.37) | data formatting | bytes 524288

commit v3 on v2

--- a/solution.py
+++ b/solution.py
@@ -22,14 +22,20 @@
 MESH = pl.DeviceIdType.MESH
 
 CHUNKS = (
-    (6, 0, 4),
-    (4, 6, 0),
-    (6, 10, 12),
-    (2, 16, 10),
-    (6, 18, 20),
-    (2, 24, 18),
+    (6, 8, 12),
+    (4, 14, 8),
+    (4, 18, 4),
+    (4, 4, 18),
+    (4, 0, 22),
+    (4, 22, 0),
     (4, 26, 28),
     (2, 30, 26),
+)
+GROUPS = (
+    ((2, 1), (2, 0)),
+    ((1, 1), (3, 0)),
+    ((3, 1), (1, 0)),
+    ((4, 1), (4, 0)),
 )
 
 
@@ -102,7 +108,7 @@
             tables.at[0, :, pl.ds(first, SUB), :], raw.at[i], load_sem.at[i]
         )
 
-    for i in range(4):
+    for i in (1, 0, 2, 3):
         load(i).start()
 
     bar = pltpu.get_barrier_semaphore()
@@ -142,18 +148,9 @@
 
         lax.fori_loop(0, DEPTH, one, 0)
 
-    load(0).wait()
-    pick(0)
-    load(3).wait()
-    pick(3)
-
-    def wrap(d, carry):
-        send[d, pl.ds(0, SUB), :] = send[d, pl.ds(32 * SUB, SUB), :]
-        return carry
-
-    lax.fori_loop(0, DEPTH, wrap, 0)
-    load(1).wait()
-    pick(1)
+    for i in (1, 0, 2):
+        load(i).wait()
+        pick(i)
 
     pl.semaphore_wait(bar, DEPTH - 1 + 4)
 
@@ -186,11 +183,17 @@
         recv[0, rows, :] = send[0, rows, :]
 
     lax.fori_loop(1, DEPTH, send_info, 0)
-    send_chunk(0)
-    send_chunk(1)
-    load(2).wait()
-    pick(2)
-    for n in range(2, 8):
+    for n in range(4):
+        send_chunk(n)
+    load(3).wait()
+    pick(3)
+
+    def wrap(d, carry):
+        send[d, pl.ds(0, SUB), :] = send[d, pl.ds(32 * SUB, SUB), :]
+        return carry
+
+    lax.fori_loop(0, DEPTH, wrap, 0)
+    for n in range(4, 8):
         send_chunk(n)
     for n in range(8):
         own_chunk(n)
@@ -240,12 +243,17 @@
 
     c0, c1, c2, c3 = coeffs
 
+    def owner_place(m, who):
+        (ahead1, half1), (ahead0, half0) = GROUPS[m]
+        return ahead0 + (ahead1 - ahead0) * who, half0 + (half1 - half0) * who
+
     def piece_rows(p):
         return pl.ds(p * (8 // PIECES), 8 // PIECES)
 
-    def partial_rows(m, half, target, p):
-        low_q = 8 * m + 4 * half
-        owner = 2 * ((z + 1 + m) % 4) + half
+    def partial_rows(m, who, target, p):
+        ahead, half = owner_place(m, who)
+        low_q = 8 * (ahead - 1) + 4 * half
+        owner = 2 * ((z + ahead) % 4) + half
         at_first = (owner == 0).astype(jnp.int32)
         at_last = (owner == 7).astype(jnp.int32)
         per = KK // PIECES
@@ -294,7 +302,8 @@
         )
 
     def to_owner(m, p):
-        far = 2 * ((z + 1 + m) % 4) + c
+        ahead, half = owner_place(m, c)
+        far = 2 * ((z + ahead) % 4) + half
         return pltpu.make_async_remote_copy(
             far_send.at[m, piece_rows(p)], far_recv.at[m, piece_rows(p)],
             far_ssem.at[m, p], far_rsem.at[m, p],

time: 44.9 us -> 43.1 us (0.960)
  the two profiles are of different devices: /device:TPU:33 before, /device:TPU:0 now
where the time goes in v3:
time: 43.1 us; the launch traced here: 42.9 us
  Pallas kernels  41.2 us (96%)
  local copies, waits for them, and re-layouts  1.67 us (4%)
    pallas_call x1, Pallas kernels, shards(): pl.pallas_call(functools.partial(kernel, sine_coefficients()), out_shape=...  41.2 us
    unnamed x1, local copies, waits for them, and re-layouts  1.67 us

profile of v3, /device:TPU:0, one launch (start us, length us, event | category | flops | bytes accessed | tf_op | source)
XLA Modules:
  0.0 42.9 jit_solution(3526306089709365516)
XLA Ops:
  0.0 41.2 %shard_map.37 = f32[2,8,32,128]{3,2,1,0:T(8,128)} custom-call(f32[1,32,32,1024]{3,2,1,0:T(8,128)} %tables.1, f32[1,32]{1,0:T(1,128)} %weights.1, s32[1,32]{1,0:T(1,128)} %aperture.1), custom_call_target="tpu_custom_call" | custom-call | tf_op jit(solution)/shard_map/pallas_call | solution.py:399
  41.3 1.7 %copy.5 = f32[2,8,32,128]{3,2,1,0:T(8,128)} copy(f32[2,8,32,128]{3,2,1,0:T(8,128)} %shard_map.37) | data formatting | bytes 524288

commit v4 on v3

--- a/solution.py
+++ b/solution.py
@@ -22,8 +22,9 @@
 MESH = pl.DeviceIdType.MESH
 
 CHUNKS = (
-    (6, 8, 12),
-    (4, 14, 8),
+    (8, 9, 9),
+    (1, 8, 8),
+    (1, 17, 17),
     (4, 18, 4),
     (4, 4, 18),
     (4, 0, 22),
@@ -31,6 +32,7 @@
     (4, 26, 28),
     (2, 30, 26),
 )
+ARRIVALS = (((0, 1, 2), ()), ((3,), (4,)), ((5,), (6,)), ((7,), (8,)))
 GROUPS = (
     ((2, 1), (2, 0)),
     ((1, 1), (3, 0)),
@@ -67,9 +69,12 @@
 def kernel(
     coeffs,
     tables,
+    weights_in,
+    aperture_in,
+    out,
     weights,
     aperture,
-    out,
+    small_sem,
     raw,
     send,
     recv,
@@ -102,15 +107,6 @@
     def owner_of(d):
         return ((tx + d // 4) % 4) * 4 + (ty + d % 4) % 4
 
-    def load(i):
-        first = pl.multiple_of(((z + 1 + i) % 4) * SUB, SUB)
-        return pltpu.make_async_copy(
-            tables.at[0, :, pl.ds(first, SUB), :], raw.at[i], load_sem.at[i]
-        )
-
-    for i in (1, 0, 2, 3):
-        load(i).start()
-
     bar = pltpu.get_barrier_semaphore()
 
     def greet(d, carry):
@@ -123,6 +119,24 @@
     for m in range(3):
         far = 2 * ((z + 1 + m) % 4) + c
         pl.semaphore_signal(bar, inc=1, device_id={"src": far, "tile": t}, device_id_type=MESH)
+
+    small = (
+        pltpu.make_async_copy(weights_in, weights, small_sem.at[0]),
+        pltpu.make_async_copy(aperture_in, aperture, small_sem.at[1]),
+    )
+    for copy in small:
+        copy.start()
+
+    def load(i):
+        first = pl.multiple_of(((z + 1 + i) % 4) * SUB, SUB)
+        return pltpu.make_async_copy(
+            tables.at[0, :, pl.ds(first, SUB), :], raw.at[i], load_sem.at[i]
+        )
+
+    load(1).start()
+
+    for copy in small:
+        copy.wait()
 
     def fill_info(d, carry):
         first = 2 * owner_of(d)
@@ -148,9 +162,10 @@
 
         lax.fori_loop(0, DEPTH, one, 0)
 
-    for i in (1, 0, 2):
-        load(i).wait()
-        pick(i)
+    load(1).wait()
+    for i in (0, 2, 3):
+        load(i).start()
+    pick(1)
 
     pl.semaphore_wait(bar, DEPTH - 1 + 4)
 
@@ -183,7 +198,13 @@
         recv[0, rows, :] = send[0, rows, :]
 
     lax.fori_loop(1, DEPTH, send_info, 0)
-    for n in range(4):
+    send_chunk(0)
+    load(0).wait()
+    pick(0)
+    send_chunk(1)
+    load(2).wait()
+    pick(2)
+    for n in (2, 3, 4):
         send_chunk(n)
     load(3).wait()
     pick(3)
@@ -193,9 +214,9 @@
         return carry
 
     lax.fori_loop(0, DEPTH, wrap, 0)
-    for n in range(4, 8):
+    for n in range(5, len(CHUNKS)):
         send_chunk(n)
-    for n in range(8):
+    for n in range(len(CHUNKS)):
         own_chunk(n)
 
     row = lax.broadcasted_iota(jnp.int32, (2 * LANES, 2 * LANES), 0)
@@ -317,13 +338,16 @@
         ).wait()
 
     for m in range(4):
-        wait_chunk(2 * m)
-        refine_rows(2 * m)
+        for n in ARRIVALS[m][0]:
+            wait_chunk(n)
+        for n in ARRIVALS[m][0]:
+            refine_rows(n)
         for p in range(PIECES):
             partial_rows(m, 1 - c, sib_send.at[m], p)
             to_sibling(m, p).start()
-        wait_chunk(2 * m + 1)
-        refine_rows(2 * m + 1)
+        for n in ARRIVALS[m][1]:
+            wait_chunk(n)
+            refine_rows(n)
         mine = far_send.at[m] if m < 3 else final
         for p in range(PIECES):
             partial_rows(m, c, mine, p)
@@ -379,7 +403,7 @@
     pltpu.make_async_copy(
         info_send_bytes, info_recv.at[pl.ds(1, DEPTH - 1)], info_ssem
     ).wait()
-    for n in range(8):
+    for n in range(len(CHUNKS)):
         rows = rows_of(n)
         pltpu.make_async_copy(
             send.at[pl.ds(1, DEPTH - 1), rows], recv.at[pl.ds(1, DEPTH - 1), rows], send_sem.at[n]
@@ -401,11 +425,14 @@
         out_shape=jax.ShapeDtypeStruct((2, 8, 2 * BY, 2 * BZ), f32),
         in_specs=[
             pl.BlockSpec(memory_space=pl.ANY),
-            pl.BlockSpec(memory_space=pltpu.SMEM),
-            pl.BlockSpec(memory_space=pltpu.SMEM),
+            pl.BlockSpec(memory_space=pl.ANY),
+            pl.BlockSpec(memory_space=pl.ANY),
         ],
         out_specs=pl.BlockSpec(memory_space=pltpu.VMEM),
         scratch_shapes=[
+            pltpu.SMEM((1, 32), f32),
+            pltpu.SMEM((1, 32), jnp.int32),
+            dma((2,)),
             vmem((4, 32, SUB, 1024), f32),
             vmem((DEPTH, 33 * SUB, LANES), f32),
             vmem((DEPTH, ROWS * SUB, LANES), f32),
@@ -421,8 +448,8 @@
             vmem(part, f32),
             vmem((2 * LANES, 2 * LANES), jnp.bfloat16),
             dma((4,)),
-            dma((8,)),
-            dma((8,)),
+            dma((len(CHUNKS),)),
+            dma((len(CHUNKS),)),
             dma,
             dma,
             dma((4, PIECES)),

time: 43.1 us -> 41.9 us (0.972)
  Pallas kernels: 41.2 us -> 40.1 us
    pallas_call x1, Pallas kernels: 41.2 us -> 40.1 us  [shards(): pl.pallas_call(functools.partial(kernel, sine_coefficients()), out_shape=...]
where the time goes in v4:
time: 41.9 us; the launch traced here: 41.7 us
  Pallas kernels  40.1 us (96%)
  local copies, waits for them, and re-layouts  1.67 us (4%)
    pallas_call x1, Pallas kernels, shards(): pl.pallas_call(functools.partial(kernel, sine_coefficients()), out_shape=...  40.1 us
    unnamed x1, local copies, waits for them, and re-layouts  1.67 us

profile of v4, /device:TPU:0, one launch (start us, length us, event | category | flops | bytes accessed | tf_op | source)
XLA Modules:
  0.0 41.7 jit_solution(11900713120469734228)
XLA Ops:
  0.0 40.1 %shard_map.37 = f32[2,8,32,128]{3,2,1,0:T(8,128)} custom-call(f32[1,32,32,1024]{3,2,1,0:T(8,128)} %tables.1, f32[1,32]{1,0:T(1,128)} %weights_in.1, s32[1,32]{1,0:T(1,128)} %aperture_in.1), custom_call_target="tpu_custom_call" | custom-call | tf_op jit(solution)/shard_map/pallas_call | solution.py:423
  40.1 1.7 %copy.5 = f32[2,8,32,128]{3,2,1,0:T(8,128)} copy(f32[2,8,32,128]{3,2,1,0:T(8,128)} %shard_map.37) | data formatting | bytes 524288

commit v5 on v4

--- a/solution.py
+++ b/solution.py
@@ -458,9 +458,9 @@
             dma((3, PIECES)),
         ],
         compiler_params=pltpu.CompilerParams(
-            collective_id=0, has_side_effects=True, vmem_limit_bytes=60 * 2**20
+            collective_id=0, has_side_effects=True, vmem_limit_bytes=51 * 2**20
         ),
-    )(tables, weights, aperture)
+    )(*(pltpu.with_memory_space_constraint(v, pltpu.HBM) for v in (tables, weights, aperture)))
 
 
 def solution(mesh):

time: 41.9 us -> 40.2 us (0.959)
  local copies, waits for them, and re-layouts: 1.67 us -> 0.71 us
  Pallas kernels: 40.1 us -> 39.3 us
    unnamed x1, local copies, waits for them, and re-layouts: 1.67 us -> 0.71 us
    pallas_call x1, Pallas kernels: 40.1 us -> 39.3 us  [shards(): pl.pallas_call(functools.partial(kernel, sine_coefficients()), out_shape=...]
where the time goes in v5:
time: 40.2 us; the launch traced here: 40.1 us
  Pallas kernels  39.3 us (98%)
  local copies, waits for them, and re-layouts  0.71 us (2%)
    pallas_call x1, Pallas kernels, shards(): pl.pallas_call(functools.partial(kernel, sine_coefficients()), out_shape=...  39.3 us

profile of v5, /device:TPU:0, one launch (start us, length us, event | category | flops | bytes accessed | tf_op | source)
XLA Modules:
  0.0 40.1 jit_solution(10389273534136494177)
XLA Ops:
  0.0 39.3 %shard_map.37 = f32[2,8,32,128]{3,2,1,0:T(8,128)S(1)} custom-call(f32[1,32,32,1024]{3,2,1,0:T(8,128)} %tables.1, f32[1,32]{1,0:T(1,128)} %weights_in.1, s32[1,32]{1,0:T(1,128)} %aperture_in.1), custom_call_target="tpu_custom_call" | custom-call | tf_op jit(solution)/shard_map/pallas_call | solution.py:423
  39.4 0.7 %copy.5 = f32[2,8,32,128]{3,2,1,0:T(8,128)} copy(f32[2,8,32,128]{3,2,1,0:T(8,128)S(1)} %shard_map.37) | data formatting | bytes 524288

commit v6 on v5

--- a/solution.py
+++ b/solution.py
@@ -143,7 +143,7 @@
         for j in range(2):
             w = jnp.full((SUB, LANES), weights[0, first + j], jnp.float32)
             live = jnp.full((SUB, LANES), aperture[0, first + j], jnp.int32)
-            info_send[d, j] = w * live.astype(jnp.float32)
+            info_send[d, pl.ds(j, 1), :] = (w * live.astype(jnp.float32))[0:1]
         return carry
 
     lax.fori_loop(0, DEPTH, fill_info, 0)
@@ -176,7 +176,7 @@
 
     def send_info(d, carry):
         pltpu.make_async_remote_copy(
-            info_send.at[d], info_recv.at[d], info_ssem, info_rsem,
+            info_send.at[d, pl.ds(0, 2)], info_recv.at[d, pl.ds(0, 2)], info_ssem, info_rsem,
             device_id={"tile": owner_of(d), "src": a}, device_id_type=MESH,
         ).start()
         return carry
@@ -197,8 +197,8 @@
         rows = rows_of(n)
         recv[0, rows, :] = send[0, rows, :]
 
+    send_chunk(0)
     lax.fori_loop(1, DEPTH, send_info, 0)
-    send_chunk(0)
     load(0).wait()
     pick(0)
     send_chunk(1)
@@ -224,12 +224,13 @@
     place = ((row // BZ) % 2) * LANES + 2 * (row % BZ) + row // LANES
     perm[...] = (col == place).astype(jnp.float32).astype(jnp.bfloat16)
 
-    info_send_bytes = info_send.at[pl.ds(1, DEPTH - 1)]
-    pltpu.make_async_copy(
-        info_send_bytes, info_recv.at[pl.ds(1, DEPTH - 1)], info_rsem
-    ).wait()
-    splat[0] = info_send[0]
-    splat[pl.ds(1, DEPTH - 1)] = info_recv[pl.ds(1, DEPTH - 1)]
+    info_out = info_send.at[pl.ds(1, DEPTH - 1), pl.ds(0, 2)]
+    info_in = info_recv.at[pl.ds(1, DEPTH - 1), pl.ds(0, 2)]
+    pltpu.make_async_copy(info_out, info_in, info_rsem).wait()
+    for s in range(DEPTH):
+        origin = info_recv if s else info_send
+        for j in range(2):
+            splat[s, j] = jnp.broadcast_to(origin[s, pl.ds(j, 1), :], (SUB, LANES))
     total_weight[...] = jnp.sum(splat[...], axis=0)
 
     def refine_rows(n):
@@ -349,6 +350,16 @@
             wait_chunk(n)
             refine_rows(n)
         mine = far_send.at[m] if m < 3 else final
+        if m == 3:
+            for k in range(2):
+                for p in range(PIECES):
+                    to_owner(k, p).wait_recv()
+
+            def add_far(x, carry):
+                far_recv[0, x] = far_recv[0, x] + far_recv[1, x]
+                return carry
+
+            lax.fori_loop(0, 8, add_far, 0)
         for p in range(PIECES):
             partial_rows(m, c, mine, p)
             to_sibling(m, p).wait_recv()
@@ -361,9 +372,8 @@
                 lax.fori_loop(p * (8 // PIECES), (p + 1) * (8 // PIECES), add_sibling, 0)
                 to_owner(m, p).start()
 
-    for m in range(3):
-        for p in range(PIECES):
-            to_owner(m, p).wait_recv()
+    for p in range(PIECES):
+        to_owner(2, p).wait_recv()
 
     for par in range(2):
 
@@ -372,8 +382,7 @@
                 for comp in range(2):
                     at = 2 * par + comp
                     got = final[x, tile, at] + sib_recv[3, x, tile, at]
-                    for m in range(3):
-                        got = got + far_recv[m, x, tile, at]
+                    got = got + far_recv[0, x, tile, at] + far_recv[2, x, tile, at]
                     final[x, tile, at] = got
             return carry
 
@@ -388,7 +397,7 @@
     for par in range(2):
         value = halves[par]
         mixed = jnp.zeros((16 * SUB, 2 * LANES), jnp.float32)
-        for _ in range(3):
+        for _ in range(2):
             part = value.astype(jnp.bfloat16)
             value = value - part.astype(jnp.float32)
             mixed = mixed + jnp.dot(part, perm[...], preferred_element_type=jnp.float32)
@@ -400,9 +409,7 @@
                         mixed[at : at + SUB, h * LANES : (h + 1) * LANES]
                     )
 
-    pltpu.make_async_copy(
-        info_send_bytes, info_recv.at[pl.ds(1, DEPTH - 1)], info_ssem
-    ).wait()
+    pltpu.make_async_copy(info_out, info_in, info_ssem).wait()
     for n in range(len(CHUNKS)):
         rows = rows_of(n)
         pltpu.make_async_copy(
@@ -436,8 +443,8 @@
             vmem((4, 32, SUB, 1024), f32),
             vmem((DEPTH, 33 * SUB, LANES), f32),
             vmem((DEPTH, ROWS * SUB, LANES), f32),
-            vmem((DEPTH, 2, SUB, LANES), f32),
-            vmem((DEPTH, 2, SUB, LANES), f32),
+            vmem((DEPTH, SUB, LANES), f32),
+            vmem((DEPTH, SUB, LANES), f32),
             vmem((DEPTH, 2, SUB, LANES), f32),
             vmem((2, SUB, LANES), f32),
             vmem((ROWS, DEPTH, COMPS, SUB, LANES), f32),

time: 40.2 us -> 39 us (0.970)
  Pallas kernels: 39.3 us -> 38.2 us
    pallas_call x1, Pallas kernels: 39.3 us -> 38.2 us  [shards(): pl.pallas_call(functools.partial(kernel, sine_coefficients()), out_shape=...]
where the time goes in v6:
time: 39 us; the launch traced here: 38.9 us
  Pallas kernels  38.2 us (98%)
  local copies, waits for them, and re-layouts  0.71 us (2%)
    pallas_call x1, Pallas kernels, shards(): pl.pallas_call(functools.partial(kernel, sine_coefficients()), out_shape=...  38.2 us

profile of v6, /device:TPU:0, one launch (start us, length us, event | category | flops | bytes accessed | tf_op | source)
XLA Modules:
  0.0 38.9 jit_solution(10021927734911480462)
XLA Ops:
  0.0 38.2 %shard_map.37 = f32[2,8,32,128]{3,2,1,0:T(8,128)S(1)} custom-call(f32[1,32,32,1024]{3,2,1,0:T(8,128)} %tables.1, f32[1,32]{1,0:T(1,128)} %weights_in.1, s32[1,32]{1,0:T(1,128)} %aperture_in.1), custom_call_target="tpu_custom_call" | custom-call | tf_op jit(solution)/shard_map/pallas_call | solution.py:430
  38.2 0.7 %copy.5 = f32[2,8,32,128]{3,2,1,0:T(8,128)} copy(f32[2,8,32,128]{3,2,1,0:T(8,128)S(1)} %shard_map.37) | data formatting | bytes 524288
